TPU v7x, 32 devices: a whole 2x2x4 slice. The times are simulated.
32 devices in a mesh: blk: 16 (over z, x, core), cat: 2 (over y).
Axes of the slice: x: 2, y: 2, z: 4, core: 2. Of those that a mesh axis runs over, the one named last changes fastest.
Arguments:
- item_content: bfloat16 [32768, 512], P('blk', 'cat'), may hold values from -6 to 6
- projection: bfloat16 [512, 256], replicated, may hold values from -0.06591797 to 0.06591797
- send_order: int32 [32, 1024], P(('blk', 'cat')), may hold values from 0 to 1023, each once within a row
- user_factors: float32 [16384, 256], P(('blk', 'cat')), may hold values from -1.5 to 1.5
- ratings: int32 [16384, 4, 1024], P(('blk', 'cat')), may hold values from 0 to 5, as said below
Outputs:
- users_out: float32 [16384, 256], P(('blk', 'cat'))
- items_out: float32 [32768, 256], P(('blk', 'cat'))
Inputs may be any that keep to these rules, and one draw needn't show every extreme that they name: `send_order`: each row is a permutation of 0 .. 1023. `ratings`: 0 means no rating, 1 to 5 a rating.
All inputs are finite; a program needn't handle non-finite values.
Results may differ from a plain program's by a relative error of at most 0.0003.
Values may be sent and summed in bfloat16 or wider, within the bound.
A program may use at most 64 MiB of HBM per device.

v0:
```python
import functools
import jax
import jax.numpy as jnp
from jax import lax
from jax.experimental import pallas as pl
from jax.experimental.pallas import tpu as pltpu
from jax.sharding import PartitionSpec as P

learn_rate = 0.004
shrink = 0.05
LEVELS = 32000.0
STEPS = 20.0
EXTRA = 16
CHUNK = 256
PARTS = 2


def split(value):
    high = value.astype(jnp.bfloat16)
    return high, (value - high.astype(jnp.float32)).astype(jnp.bfloat16)


def product(left, right, dims):
    def one(a, b):
        return lax.dot_general(a, b, (dims, ((), ())), preferred_element_type=jnp.float32)

    return one(left[0], right[0]) + (one(left[0], right[1]) + one(left[1], right[0]))


def code_of(largest):
    return jnp.ceil(jnp.log(jnp.maximum(largest, 1e-30)) * STEPS)


def step_of(code):
    return jnp.exp(code * (1.0 / STEPS)) * (1.0 / LEVELS)


def coded(value, step):
    return jnp.floor(value * (1.0 / step) + 0.5).astype(jnp.int32).astype(jnp.int16)


def unpack_kernel(in_ref, *out_refs):
    for t, out_ref in enumerate(out_refs):
        out_ref[...] = in_ref[:, t, :].astype(jnp.float32).astype(jnp.bfloat16)


def unpack(ratings):
    users, rounds, items = ratings.shape
    block = min(64, users)
    return pl.pallas_call(
        unpack_kernel,
        grid=(users // block,),
        in_specs=[pl.BlockSpec((block, rounds, items), lambda i: (i, 0, 0))],
        out_specs=[pl.BlockSpec((block, items), lambda i: (i, 0))] * rounds,
        out_shape=[jax.ShapeDtypeStruct((users, items), jnp.bfloat16)] * rounds,
        cost_estimate=pl.CostEstimate(
            flops=1000 * ratings.size, bytes_accessed=6 * ratings.size, transcendentals=0
        ),
        name="unpack",
    )(ratings)


def round_kernel(
    packed_in, packed_out, first, last, users_ref, items_ref, values_ref, grad_ref, users_out, items_out
):
    items, rank = values_ref.shape[1], users_ref.shape[1]
    users = users_ref[...]
    user_parts = split(users)
    chunk = min(CHUNK, items)
    user_grad = jnp.zeros(users.shape, jnp.float32) if first else grad_ref[...]
    if packed_in:
        steps_in = step_of(items_ref[items:, :].astype(jnp.int32).astype(jnp.float32))
    if packed_out:
        row = lax.broadcasted_iota(jnp.int32, (EXTRA, rank), 0)
        codes = jnp.zeros((EXTRA, rank), jnp.float32)
    for n in range(items // chunk):
        at = pl.ds(n * chunk, chunk)
        old = items_ref[at, :]
        if packed_in:
            old = old.astype(jnp.int32).astype(jnp.float32) * steps_in[n : n + 1, :]
        old_parts = split(old)
        guess = product(user_parts, old_parts, ((1,), (1,)))
        values = values_ref[:, at].astype(jnp.float32)
        errors = jnp.where(values > 0.0, values - guess, 0.0)
        error_parts = split(errors)
        item_grad = product(error_parts, user_parts, ((0,), (0,)))
        new = old + learn_rate * (item_grad - shrink * old)
        if packed_out:
            code = code_of(jnp.max(jnp.abs(new), axis=0, keepdims=True))
            codes = jnp.where(row == n, code, codes)
            items_out[at, :] = coded(new, step_of(code))
        else:
            items_out[at, :] = new
        user_grad += product(error_parts, old_parts, ((1,), (0,)))
    if packed_out:
        items_out[pl.ds(items, EXTRA), :] = codes.astype(jnp.int32).astype(jnp.int16)
    if last:
        user_grad = users + learn_rate * (user_grad - shrink * users)
    users_out[...] = user_grad


def update(users, items, values, grad, part, packed_in, packed_out):
    n_users, rank = users.shape
    n_items = values.shape[1] // PARTS
    whole = lambda shape: pl.BlockSpec(shape, lambda i: (0, 0))
    out_items = (
        jax.ShapeDtypeStruct((n_items + EXTRA, rank), jnp.int16)
        if packed_out
        else jax.ShapeDtypeStruct((n_items, rank), jnp.float32)
    )
    return pl.pallas_call(
        functools.partial(round_kernel, packed_in, packed_out, part == 0, part == PARTS - 1),
        grid=(1,),
        in_specs=[
            whole(users.shape),
            whole(items.shape),
            pl.BlockSpec((n_users, n_items), lambda i: (0, part)),
            whole(users.shape),
        ],
        out_specs=[whole(users.shape), whole(out_items.shape)],
        out_shape=[jax.ShapeDtypeStruct(users.shape, jnp.float32), out_items],
        cost_estimate=pl.CostEstimate(
            flops=18 * n_users * n_items * rank, bytes_accessed=5 << 20, transcendentals=0
        ),
        compiler_params=pltpu.CompilerParams(vmem_limit_bytes=48 << 20),
        name="sgd_round",
    )(users, items, values, grad)


def project(item_content, projection):
    def dot(rows, weights):
        return jnp.dot(rows, weights, preferred_element_type=jnp.float32)

    if lax.axis_size("cat") != 2:
        rows = lax.all_to_all(item_content, "cat", split_axis=0, concat_axis=1, tiled=True)
        return dot(rows, projection)
    me = lax.axis_index("cat")
    rows, width = item_content.shape[0] // 2, item_content.shape[1]
    other = 1 - me
    theirs = lax.dynamic_slice_in_dim(item_content, other * rows, rows)
    got = lax.ppermute(theirs, "cat", [(0, 1), (1, 0)])
    mine = lax.dynamic_slice_in_dim(item_content, me * rows, rows)
    near = dot(mine, lax.dynamic_slice_in_dim(projection, me * width, width))
    return near + dot(got, lax.dynamic_slice_in_dim(projection, other * width, width))


def body(item_content, projection, send_order, user_factors, ratings):
    size = lax.axis_size("blk")
    rounds = ratings.shape[1]
    values = unpack(ratings)
    owned = project(item_content, projection)
    ordered = owned.at[send_order[0]].get(mode="promise_in_bounds")
    dealt = ordered.reshape(size, -1, ordered.shape[1])
    share = dealt.shape[1]
    code = code_of(jnp.max(jnp.abs(dealt), axis=1, keepdims=True))
    sent = jnp.concatenate(
        [coded(dealt, step_of(code)), code.astype(jnp.int32).astype(jnp.int16)], axis=1
    )
    got = lax.all_to_all(sent, "blk", split_axis=0, concat_axis=0, tiled=True)
    got = got.astype(jnp.int32).astype(jnp.float32)
    items = (got[:, :share] * step_of(got[:, share:])).reshape(owned.shape)
    users = user_factors
    ring = [(i, (i + 1) % size) for i in range(size)]
    parts = jnp.split(items, PARTS)
    for t in range(rounds):
        grad = users
        sent = []
        for part in range(PARTS):
            grad, moved = update(
                users, parts[part], values[t], grad, part, t > 0, t < rounds - 1
            )
            sent.append(lax.ppermute(moved, "blk", ring) if t < rounds - 1 else moved)
        users, parts = grad, sent
    return (users, jnp.concatenate(parts))


def solution(mesh):
    placed = (
        P("blk", "cat"),
        P(),
        P(("blk", "cat"), None),
        P(("blk", "cat"), None),
        P(("blk", "cat"), None, None),
    )
    return jax.shard_map(
        body,
        mesh=mesh,
        in_specs=placed,
        out_specs=(P(("blk", "cat"), None), P(("blk", "cat"), None)),
        check_vma=False,
    )
```

profile of v0, /device:TPU:0, one launch (start us, length us, event | category | flops | bytes accessed | tf_op | source)
XLA Modules:
  0.0 84.6 jit_solution(5607522023987395920)
XLA Ops:
  0.6 0.0 copy-start
  0.6 1.2 %copy-done = bf16[2048,256]{1,0:T(8,128)(2,1)S(1)} copy-done((bf16[2048,256]{1,0:T(8,128)(2,1)S(1)}, bf16[2048,256]{1,0:T(8,128)(2,1)}, u32[]{:S(2)}) %copy-start) | copy-done | bytes 1048600
  1.9 0.0 copy-start.7
  1.9 0.0 copy-start.6
  1.9 3.1 %collective-permute-start = (bf16[1024,256]{1,0:T(8,128)(2,1)S(1)}, bf16[1024,256]{1,0:T(8,128)(2,1)S(1)}, u32[]{:S(2)}, u32[]{:S(2)}) collective-permute-start(bf16[1024,256]{1,0:T(8,128)(2,1)S(1)} %constant_dynamic-slice_fusion), channel_id=1, source_target_pairs={{0,1},{1,0},{2,3},{3,2},{4,5},{5,4},{6,7},{7,6},{8,9},{9,8},{10,11... | collective-permute-start | bytes 1572872 | tf_op jit(solution)/shard_map/ppermute | solution.py:141
  5.0 1.2 %fusion = f32[1024,256]{1,0:T(8,128)S(1)} fusion(bf16[2048,256]{1,0:T(8,128)(2,1)S(1)} %copy-done, s32[]{:T(128)S(6)} %select_n.22, bf16[512,256]{1,0:T(8,128)(2,1)} %param.6, s32[]{:T(128)S(6)} %select_n.23), kind=kOutput, calls=%fused_computation.8 | convolution fusion | flops 134217728 | bytes 1703944 | tf_op jit(solution)/shard_map/dot_general | solution.py:132
  6.2 0.0 copy-done.7
  6.2 10.7 %collective-permute-done = bf16[1024,256]{1,0:T(8,128)(2,1)S(1)} collective-permute-done((bf16[1024,256]{1,0:T(8,128)(2,1)S(1)}, bf16[1024,256]{1,0:T(8,128)(2,1)S(1)}, u32[]{:S(2)}, u32[]{:S(2)}) %collective-permute-start) | collective-permute-done | bytes 524320 | tf_op jit(solution)/shard_map/ppermute | solution.py:141
  16.9 0.0 copy-done.6
  16.9 0.3 convolution_add_fusion
  17.2 3.5 %gather_fusion = f32[1024,256]{1,0:T(8,128)S(1)} fusion(f32[1024,256]{1,0:T(8,128)S(1)} %convolution_add_fusion, s32[1024]{0:T(1024)S(1)} %broadcast_clamp_fusion), kind=kCustom, calls=%fused_computation | custom fusion | bytes 2101248 | tf_op jit(solution)/shard_map/gather | solution.py:152
  20.7 0.1 abs_reduce_fusion
  20.8 0.2 convert_convert_fusion.1
  21.0 0.9 %pad_add_fusion = s16[16,65,256]{2,1,0:T(8,128)(2,1)} fusion(s16[16,1,256]{2,1,0:T(2,128)(2,1)S(1)} %copy.7, s16[16,64,256]{2,1,0:T(8,128)(2,1)S(1)} %convert_convert_fusion.1), kind=kLoop, calls=%fused_computation.7 | loop fusion | flops 266240 | bytes 1064960 | tf_op jit(solution)/shard_map/concatenate | solution.py:156
  21.9 6.1 %all-to-all-start = ((s16[16,65,256]{2,1,0:T(8,128)(2,1)}), s16[16,65,256]{2,1,0:T(8,128)(2,1)S(1)}, u32[]{:S(2)}, u32[]{:S(2)}) async-start(s16[16,65,256]{2,1,0:T(8,128)(2,1)} %pad_add_fusion), calls=%async_computation | async-start | bytes 1179648 | tf_op jit(solution)/shard_map/all_to_all | solution.py:159
  28.0 12.7 %unpack.1 = (bf16[512,1024]{1,0:T(8,128)(2,1)}, bf16[512,1024]{1,0:T(8,128)(2,1)}, bf16[512,1024]{1,0:T(8,128)(2,1)}, bf16[512,1024]{1,0:T(8,128)(2,1)}) custom-call(s32[512,4,1024]{2,1,0:T(4,128)} %in_ref.1), custom_call_target="tpu_custom_call" | custom-call | flops 2097152000 | bytes 12582912 | tf_op jit(solution)/shard_map/unpack/pallas_call | solution.py:50
  40.8 2.6 %all-to-all-done = s16[16,65,256]{2,1,0:T(8,128)(2,1)S(1)} async-done(((s16[16,65,256]{2,1,0:T(8,128)(2,1)}), s16[16,65,256]{2,1,0:T(8,128)(2,1)S(1)}, u32[]{:S(2)}, u32[]{:S(2)}) %all-to-all-start) | async-done | bytes 532512 | tf_op jit(solution)/shard_map/all_to_all | solution.py:159
  43.4 0.2 convert_convert_fusion
  43.6 0.1 slice_multiply_fusion
  43.7 0.0 copy-start.4
  43.7 0.0 copy-start.5
  43.8 0.1 fusion.9
  43.9 1.1 %copy-done.4 = bf16[512,1024]{1,0:T(8,128)(2,1)S(1)} copy-done((bf16[512,1024]{1,0:T(8,128)(2,1)S(1)}, bf16[512,1024]{1,0:T(8,128)(2,1)}, u32[]{:S(2)}) %copy-start.4) | copy-done | bytes 1048600
  45.0 0.1 copy-done.5
  45.1 2.2 %sgd_round.8 = (f32[512,256]{1,0:T(8,128)S(1)}, s16[528,256]{1,0:T(8,128)(2,1)S(1)}) custom-call(f32[512,256]{1,0:T(8,128)S(1)} %copy-done.5, f32[512,256]{1,0:T(8,128)S(1)} %bitcast.15, bf16[512,1024]{1,0:T(8,128)(2,1)S(1)} %copy-done.4, f32[512,256]{1,0:T(8,128)S(1)} %copy-done.5), custom_call_target="tpu_custom_call" | custom-call | flops 1207959552 | bytes 5242880 | tf_op jit(solution)/shard_map/sgd_round/pallas_call | solution.py:111
  47.3 0.3 collective-permute-start.2
  47.5 2.2 %sgd_round.9 = (f32[512,256]{1,0:T(8,128)S(1)}, s16[528,256]{1,0:T(8,128)(2,1)S(1)}) custom-call(f32[512,256]{1,0:T(8,128)S(1)} %copy-done.5, f32[512,256]{1,0:T(8,128)S(1)} %bitcast.14, bf16[512,1024]{1,0:T(8,128)(2,1)S(1)} %copy-done.4, f32[512,256]{1,0:T(8,128)S(1)} %get-tuple-element.23.grad_ref), custom_call_target="tpu_custom_call" | custom-call | flops 1207959552 | bytes 5242880 | tf_op jit(solution)/shard_map/sgd_round/pallas_call | solution.py:111
  49.7 0.6 collective-permute-start.1
  50.3 5.6 %collective-permute-done.2.items_ref = s16[528,256]{1,0:T(8,128)(2,1)S(1)} collective-permute-done((s16[528,256]{1,0:T(8,128)(2,1)S(1)}, s16[528,256]{1,0:T(8,128)(2,1)S(1)}, u32[]{:S(2)}, u32[]{:S(2)}) %collective-permute-start.2) | collective-permute-done | bytes 270368 | tf_op jit(solution)/shard_map/ppermute | solution.py:172
  55.9 0.0 copy-done.3
  55.9 2.2 %sgd_round.10 = (f32[512,256]{1,0:T(8,128)S(1)}, s16[528,256]{1,0:T(8,128)(2,1)S(1)}) custom-call(f32[512,256]{1,0:T(8,128)S(1)} %get-tuple-element.24.users_ref.grad_ref, s16[528,256]{1,0:T(8,128)(2,1)S(1)} %collective-permute-done.2.items_ref, bf16[512,1024]{1,0:T(8,128)(2,1)S(1)} %copy-done.3, f32[512,256]{1,0:T(8,128)S(1)} %get-tuple-element.24.users_ref.grad_ref), custom_call_target="tpu_custom_call" | custom-call | flops 1207959552 | bytes 5242880 | tf_op jit(solution)/shard_map/sgd_round/pallas_call | solution.py:111
  58.1 0.1 collective-permute-start.4
  58.1 0.7 collective-permute-done.1.items_ref
  58.8 2.2 %sgd_round.11 = (f32[512,256]{1,0:T(8,128)S(1)}, s16[528,256]{1,0:T(8,128)(2,1)S(1)}) custom-call(f32[512,256]{1,0:T(8,128)S(1)} %get-tuple-element.24.users_ref.grad_ref, s16[528,256]{1,0:T(8,128)(2,1)S(1)} %collective-permute-done.1.items_ref, bf16[512,1024]{1,0:T(8,128)(2,1)S(1)} %copy-done.3, f32[512,256]{1,0:T(8,128)S(1)} %get-tuple-element.28.grad_ref), custom_call_target="tpu_custom_call" | custom-call | flops 1207959552 | bytes 5242880 | tf_op jit(solution)/shard_map/sgd_round/pallas_call | solution.py:111
  61.0 0.2 collective-permute-start.3
  61.2 5.5 %collective-permute-done.4.items_ref = s16[528,256]{1,0:T(8,128)(2,1)S(1)} collective-permute-done((s16[528,256]{1,0:T(8,128)(2,1)S(1)}, s16[528,256]{1,0:T(8,128)(2,1)S(1)}, u32[]{:S(2)}, u32[]{:S(2)}) %collective-permute-start.4) | collective-permute-done | bytes 270368 | tf_op jit(solution)/shard_map/ppermute | solution.py:172
  66.7 0.0 copy-done.2
  66.7 2.2 %sgd_round.12 = (f32[512,256]{1,0:T(8,128)S(1)}, s16[528,256]{1,0:T(8,128)(2,1)S(1)}) custom-call(f32[512,256]{1,0:T(8,128)S(1)} %get-tuple-element.29.users_ref.grad_ref, s16[528,256]{1,0:T(8,128)(2,1)S(1)} %collective-permute-done.4.items_ref, bf16[512,1024]{1,0:T(8,128)(2,1)S(1)} %copy-done.2, f32[512,256]{1,0:T(8,128)S(1)} %get-tuple-element.29.users_ref.grad_ref), custom_call_target="tpu_custom_call" | custom-call | flops 1207959552 | bytes 5242880 | tf_op jit(solution)/shard_map/sgd_round/pallas_call | solution.py:111
  68.9 0.1 collective-permute-start.6
  68.9 0.8 collective-permute-done.3.items_ref
  69.8 2.2 %sgd_round.13 = (f32[512,256]{1,0:T(8,128)S(1)}, s16[528,256]{1,0:T(8,128)(2,1)S(1)}) custom-call(f32[512,256]{1,0:T(8,128)S(1)} %get-tuple-element.29.users_ref.grad_ref, s16[528,256]{1,0:T(8,128)(2,1)S(1)} %collective-permute-done.3.items_ref, bf16[512,1024]{1,0:T(8,128)(2,1)S(1)} %copy-done.2, f32[512,256]{1,0:T(8,128)S(1)} %get-tuple-element.33.grad_ref), custom_call_target="tpu_custom_call" | custom-call | flops 1207959552 | bytes 5242880 | tf_op jit(solution)/shard_map/sgd_round/pallas_call | solution.py:111
  72.0 0.1 collective-permute-start.5
  72.0 5.5 %collective-permute-done.6.items_ref = s16[528,256]{1,0:T(8,128)(2,1)S(1)} collective-permute-done((s16[528,256]{1,0:T(8,128)(2,1)S(1)}, s16[528,256]{1,0:T(8,128)(2,1)S(1)}, u32[]{:S(2)}, u32[]{:S(2)}) %collective-permute-start.6) | collective-permute-done | bytes 270368 | tf_op jit(solution)/shard_map/ppermute | solution.py:172
  77.5 0.0 copy-done.1
  77.5 2.1 %sgd_round.14 = (f32[512,256]{1,0:T(8,128)S(1)}, f32[512,256]{1,0:T(8,128)S(1)}) custom-call(f32[512,256]{1,0:T(8,128)S(1)} %get-tuple-element.34.users_ref.grad_ref, s16[528,256]{1,0:T(8,128)(2,1)S(1)} %collective-permute-done.6.items_ref, bf16[512,1024]{1,0:T(8,128)(2,1)S(1)} %copy-done.1, f32[512,256]{1,0:T(8,128)S(1)} %get-tuple-element.34.users_ref.grad_ref), custom_call_target="tpu_custom_call" | custom-call | flops 1207959552 | bytes 5242880 | tf_op jit(solution)/shard_map/sgd_round/pallas_call | solution.py:111
  79.6 1.0 %collective-permute-done.5.items_ref = s16[528,256]{1,0:T(8,128)(2,1)S(1)} collective-permute-done((s16[528,256]{1,0:T(8,128)(2,1)S(1)}, s16[528,256]{1,0:T(8,128)(2,1)S(1)}, u32[]{:S(2)}, u32[]{:S(2)}) %collective-permute-start.5) | collective-permute-done | bytes 270368 | tf_op jit(solution)/shard_map/ppermute | solution.py:172
  80.6 2.9 %sgd_round.15 = (f32[512,256]{1,0:T(8,128)}, f32[512,256]{1,0:T(8,128)S(1)}) custom-call(f32[512,256]{1,0:T(8,128)S(1)} %get-tuple-element.34.users_ref.grad_ref, s16[528,256]{1,0:T(8,128)(2,1)S(1)} %collective-permute-done.5.items_ref, bf16[512,1024]{1,0:T(8,128)(2,1)S(1)} %copy-done.1, f32[512,256]{1,0:T(8,128)S(1)} %get-tuple-element.38.grad_ref), custom_call_target="tpu_custom_call" | custom-call | flops 1207959552 | bytes 5242880 | tf_op jit(solution)/shard_map/sgd_round/pallas_call | solution.py:111
  83.5 1.0 %pad_maximum_fusion = f32[1024,256]{1,0:T(8,128)} fusion(f32[512,256]{1,0:T(8,128)S(1)} %get-tuple-element.41, f32[512,256]{1,0:T(8,128)S(1)} %get-tuple-element.40), kind=kLoop, calls=%fused_computation.4 | loop fusion | flops 262144 | bytes 2097152 | tf_op jit(solution)/shard_map/concatenate | solution.py:174
  (10 shorter events, 0.1 us)
Async XLA Ops:
  0.6 1.2 %copy-start = (bf16[2048,256]{1,0:T(8,128)(2,1)S(1)}, bf16[2048,256]{1,0:T(8,128)(2,1)}, u32[]{:S(2)}) copy-start(bf16[2048,256]{1,0:T(8,128)(2,1)} %param.5) | copy-start | bytes 3145732
  1.9 4.3 %copy-start.7 = (s32[1,1024]{1,0:T(1,128)S(1)}, s32[1,1024]{1,0:T(1,128)}, u32[]{:S(2)}) copy-start(s32[1,1024]{1,0:T(1,128)} %param.7) | copy-start | bytes 12292
  1.9 15.0 %copy-start.6 = (bf16[512,256]{1,0:T(8,128)(2,1)S(1)}, bf16[512,256]{1,0:T(8,128)(2,1)}, u32[]{:S(2)}) copy-start(bf16[512,256]{1,0:T(8,128)(2,1)} %param.6) | copy-start | bytes 786436
  1.9 15.0 %collective-permute-start = (bf16[1024,256]{1,0:T(8,128)(2,1)S(1)}, bf16[1024,256]{1,0:T(8,128)(2,1)S(1)}, u32[]{:S(2)}, u32[]{:S(2)}) collective-permute-start(bf16[1024,256]{1,0:T(8,128)(2,1)S(1)} %constant_dynamic-slice_fusion), channel_id=1, source_target_pairs={{0,1},{1,0},{2,3},{3,2},{4,5},{5,4},{6,7},{7,6},{8,9},{9,8},{10,11... | collective-permute-start | bytes 1572872 | tf_op jit(solution)/shard_map/ppermute | solution.py:141
  21.9 21.5 %all-to-all-start = ((s16[16,65,256]{2,1,0:T(8,128)(2,1)}), s16[16,65,256]{2,1,0:T(8,128)(2,1)S(1)}, u32[]{:S(2)}, u32[]{:S(2)}) async-start(s16[16,65,256]{2,1,0:T(8,128)(2,1)} %pad_add_fusion), calls=%async_computation | async-start | bytes 1179648 | tf_op jit(solution)/shard_map/all_to_all | solution.py:159
  43.7 1.2 %copy-start.4 = (bf16[512,1024]{1,0:T(8,128)(2,1)S(1)}, bf16[512,1024]{1,0:T(8,128)(2,1)}, u32[]{:S(2)}) copy-start(bf16[512,1024]{1,0:T(8,128)(2,1)} %get-tuple-element.22.values_ref) | copy-start | bytes 3145732
  43.7 1.3 %copy-start.5 = (f32[512,256]{1,0:T(8,128)S(1)}, f32[512,256]{1,0:T(8,128)}, u32[]{:S(2)}) copy-start(f32[512,256]{1,0:T(8,128)} %users_ref.3) | copy-start | bytes 1572868
  47.3 8.6 %collective-permute-start.2 = (s16[528,256]{1,0:T(8,128)(2,1)S(1)}, s16[528,256]{1,0:T(8,128)(2,1)S(1)}, u32[]{:S(2)}, u32[]{:S(2)}) collective-permute-start(s16[528,256]{1,0:T(8,128)(2,1)S(1)} %get-tuple-element.27), channel_id=1, source_target_pairs={{0,2},{2,4},{4,6},{6,8},{8,10},{10,12},{12,14},{14,16},{16,18},{18... | collective-permute-start | bytes 811016 | tf_op jit(solution)/shard_map/ppermute | solution.py:172
  47.5 8.4 %copy-start.3 = (bf16[512,1024]{1,0:T(8,128)(2,1)S(1)}, bf16[512,1024]{1,0:T(8,128)(2,1)}, u32[]{:S(2)}) copy-start(bf16[512,1024]{1,0:T(8,128)(2,1)} %get-tuple-element.26.values_ref) | copy-start | bytes 3145732
  49.7 9.1 %collective-permute-start.1 = (s16[528,256]{1,0:T(8,128)(2,1)S(1)}, s16[528,256]{1,0:T(8,128)(2,1)S(1)}, u32[]{:S(2)}, u32[]{:S(2)}) collective-permute-start(s16[528,256]{1,0:T(8,128)(2,1)S(1)} %get-tuple-element.25), channel_id=1, source_target_pairs={{0,2},{2,4},{4,6},{6,8},{8,10},{10,12},{12,14},{14,16},{16,18},{18... | collective-permute-start | bytes 811016 | tf_op jit(solution)/shard_map/ppermute | solution.py:172
  58.1 8.6 %collective-permute-start.4 = (s16[528,256]{1,0:T(8,128)(2,1)S(1)}, s16[528,256]{1,0:T(8,128)(2,1)S(1)}, u32[]{:S(2)}, u32[]{:S(2)}) collective-permute-start(s16[528,256]{1,0:T(8,128)(2,1)S(1)} %get-tuple-element.32), channel_id=1, source_target_pairs={{0,2},{2,4},{4,6},{6,8},{8,10},{10,12},{12,14},{14,16},{16,18},{18... | collective-permute-start | bytes 811016 | tf_op jit(solution)/shard_map/ppermute | solution.py:172
  58.8 7.9 %copy-start.2 = (bf16[512,1024]{1,0:T(8,128)(2,1)S(1)}, bf16[512,1024]{1,0:T(8,128)(2,1)}, u32[]{:S(2)}) copy-start(bf16[512,1024]{1,0:T(8,128)(2,1)} %get-tuple-element.31.values_ref) | copy-start | bytes 3145732
  61.0 8.8 %collective-permute-start.3 = (s16[528,256]{1,0:T(8,128)(2,1)S(1)}, s16[528,256]{1,0:T(8,128)(2,1)S(1)}, u32[]{:S(2)}, u32[]{:S(2)}) collective-permute-start(s16[528,256]{1,0:T(8,128)(2,1)S(1)} %get-tuple-element.30), channel_id=1, source_target_pairs={{0,2},{2,4},{4,6},{6,8},{8,10},{10,12},{12,14},{14,16},{16,18},{18... | collective-permute-start | bytes 811016 | tf_op jit(solution)/shard_map/ppermute | solution.py:172
  68.9 8.6 %collective-permute-start.6 = (s16[528,256]{1,0:T(8,128)(2,1)S(1)}, s16[528,256]{1,0:T(8,128)(2,1)S(1)}, u32[]{:S(2)}, u32[]{:S(2)}) collective-permute-start(s16[528,256]{1,0:T(8,128)(2,1)S(1)} %get-tuple-element.37), channel_id=1, source_target_pairs={{0,2},{2,4},{4,6},{6,8},{8,10},{10,12},{12,14},{14,16},{16,18},{18... | collective-permute-start | bytes 811016 | tf_op jit(solution)/shard_map/ppermute | solution.py:172
  69.8 7.7 %copy-start.1 = (bf16[512,1024]{1,0:T(8,128)(2,1)S(1)}, bf16[512,1024]{1,0:T(8,128)(2,1)}, u32[]{:S(2)}) copy-start(bf16[512,1024]{1,0:T(8,128)(2,1)} %get-tuple-element.36.values_ref) | copy-start | bytes 3145732
  72.0 8.6 %collective-permute-start.5 = (s16[528,256]{1,0:T(8,128)(2,1)S(1)}, s16[528,256]{1,0:T(8,128)(2,1)S(1)}, u32[]{:S(2)}, u32[]{:S(2)}) collective-permute-start(s16[528,256]{1,0:T(8,128)(2,1)S(1)} %get-tuple-element.35), channel_id=1, source_target_pairs={{0,2},{2,4},{4,6},{6,8},{8,10},{10,12},{12,14},{14,16},{16,18},{18... | collective-permute-start | bytes 811016 | tf_op jit(solution)/shard_map/ppermute | solution.py:172
where the time goes:
time: 84.9 us; the launch traced here: 84.6 us
  waiting for transfers between devices  32.3 us (38%)
  Pallas kernels  30.8 us (36%)
  starting transfers between devices  10.4 us (12%)
  local copies, waits for them, and re-layouts  6.09 us (7%)
  other arithmetic  2.53 us (3%)
  matrix products  1.5 us (2%)
  between operations  0.87 us (1%)
    ppermute x6, waiting for transfers between devices, body(): sent.append(lax.ppermute(moved, 'blk', ring) if t < rounds - 1 else moved)  19 us
    pallas_call x8, Pallas kernels, update(): pl.pallas_call(functools.partial(round_kernel, packed_in, packed_out, par...  18.1 us
    pallas_call x1, Pallas kernels, unpack(): pl.pallas_call(unpack_kernel, grid=(users // block,), in_specs=[pl.BlockS...  12.7 us
    ppermute x1, waiting for transfers between devices, project(): got = lax.ppermute(theirs, 'cat', [(0, 1), (1, 0)])  10.7 us
    all_to_all x1, starting transfers between devices, body(): got = lax.all_to_all(sent, 'blk', split_axis=0, concat_axis=0, tiled=True)  6.13 us
    gather x1, local copies, waits for them, and re-layouts, body(): ordered = owned.at[send_order[0]].get(mode='promise_in_bounds')  3.47 us
    ppermute x1, starting transfers between devices, project(): got = lax.ppermute(theirs, 'cat', [(0, 1), (1, 0)])  3.06 us
    all_to_all x1, waiting for transfers between devices, body(): got = lax.all_to_all(sent, 'blk', split_axis=0, concat_axis=0, tiled=True)  2.63 us
  transfers between devices with their start and end apart: 8, of which 8 were waited for; matrix products, arithmetic and copies ran while one was open for 1% of the time, Pallas kernels for 30%

commit v1 on v0

v1 whole, which is shorter than its diff:
```python
import functools
import jax
import jax.numpy as jnp
from jax import lax
from jax.experimental import pallas as pl
from jax.experimental.pallas import tpu as pltpu
from jax.sharding import PartitionSpec as P

learn_rate = 0.004
shrink = 0.05
LEVELS = 32000.0
STEPS = 20.0
CHUNK = 256
LANES = 128
MESH = pl.DeviceIdType.MESH


def split(value):
    high = value.astype(jnp.bfloat16)
    return high, (value - high.astype(jnp.float32)).astype(jnp.bfloat16)


def product(left, right, dims):
    def one(a, b):
        return lax.dot_general(a, b, (dims, ((), ())), preferred_element_type=jnp.float32)

    return one(left[0], right[0]) + (one(left[0], right[1]) + one(left[1], right[0]))


def code_of(largest):
    return jnp.ceil(jnp.log(jnp.maximum(largest, 1e-30)) * STEPS)


def step_of(code):
    return jnp.exp(code * (1.0 / STEPS)) * (1.0 / LEVELS)


def coded(value, step):
    return jnp.floor(value * (1.0 / step) + 0.5).astype(jnp.int32).astype(jnp.int16)


def decoded(value, step):
    return value.astype(jnp.int32).astype(jnp.float32) * step


def rounds_kernel(
    rounds, items_in, users_in, ratings_in, users_out, items_out,
    users, ratings, sent, sent_steps, got, got_steps, load_sem, send_sem, recv_sem,
):
    size = lax.axis_size("blk")
    me = lax.axis_index("blk")
    right, left = lax.rem(me + 1, size), lax.rem(me + size - 1, size)
    n_users, rank = users.shape
    n_items = items_in.shape[0]
    chunk = got.shape[2]
    tiles = n_items // LANES
    loads = [
        pltpu.make_async_copy(users_in, users, load_sem.at[0]),
        pltpu.make_async_copy(ratings_in, ratings, load_sem.at[1]),
    ]
    for load in loads:
        load.start()
    barrier = pltpu.get_barrier_semaphore()
    pl.semaphore_signal(barrier, inc=1, device_id={"blk": left}, device_id_type=MESH)
    pl.semaphore_wait(barrier, 1)
    for load in loads:
        load.wait()

    def moves(t, n):
        return [
            pltpu.make_async_remote_copy(
                src_ref=src.at[t, n],
                dst_ref=dst.at[t, n],
                send_sem=send_sem.at[t, n, k],
                recv_sem=recv_sem.at[t, n, k],
                device_id={"blk": right},
                device_id_type=MESH,
            )
            for k, (src, dst) in enumerate([(sent, got), (sent_steps, got_steps)])
        ]

    for t in range(rounds):
        now = users[...]
        user_parts = split(now)
        user_grad = jnp.zeros(now.shape, jnp.float32)
        for n in range(n_items // chunk):
            at = pl.ds(n * chunk, chunk)
            if t == 0:
                old = items_in[at, :]
            else:
                for move in moves(t - 1, n):
                    move.wait_recv()
                old = decoded(got[t - 1, n], got_steps[t - 1, n])
            old_parts = split(old)
            guess = product(user_parts, old_parts, ((1,), (1,)))
            values = jnp.concatenate(
                [
                    ratings[pl.ds((n * (chunk // LANES) + j) * rounds + t, n_users, stride=tiles * rounds), :]
                    for j in range(chunk // LANES)
                ],
                axis=1,
            ).astype(jnp.float32)
            errors = jnp.where(values > 0.0, values - guess, 0.0)
            error_parts = split(errors)
            item_grad = product(error_parts, user_parts, ((0,), (0,)))
            new = old + learn_rate * (item_grad - shrink * old)
            if t < rounds - 1:
                step = jnp.maximum(jnp.max(jnp.abs(new), axis=0, keepdims=True), 1e-30) * (1.0 / LEVELS)
                sent[t, n] = coded(new, step)
                sent_steps[t, n] = step
                for move in moves(t, n):
                    move.start()
            else:
                items_out[at, :] = new
            user_grad += product(error_parts, old_parts, ((1,), (0,)))
        now = now + learn_rate * (user_grad - shrink * now)
        if t < rounds - 1:
            users[...] = now
        else:
            users_out[...] = now
    for t in range(rounds - 1):
        for n in range(n_items // chunk):
            for move in moves(t, n):
                move.wait_send()


def all_rounds(items, users, ratings):
    n_users, rounds, n_items = ratings.shape
    rank = users.shape[1]
    chunk = min(CHUNK, n_items)
    chunks = n_items // chunk
    view = ratings.reshape(n_users, rounds, n_items // LANES, LANES).transpose(0, 2, 1, 3).reshape(-1, LANES)
    return pl.pallas_call(
        functools.partial(rounds_kernel, rounds),
        in_specs=[
            pl.BlockSpec(memory_space=pltpu.VMEM),
            pl.BlockSpec(memory_space=pl.ANY),
            pl.BlockSpec(memory_space=pl.ANY),
        ],
        out_specs=[pl.BlockSpec(memory_space=pltpu.VMEM)] * 2,
        out_shape=[
            jax.ShapeDtypeStruct(users.shape, jnp.float32),
            jax.ShapeDtypeStruct(items.shape, jnp.float32),
        ],
        scratch_shapes=[
            pltpu.VMEM(users.shape, jnp.float32),
            pltpu.VMEM(view.shape, jnp.int32),
            pltpu.VMEM((rounds - 1, chunks, chunk, rank), jnp.int16),
            pltpu.VMEM((rounds - 1, chunks, 1, rank), jnp.float32),
            pltpu.VMEM((rounds - 1, chunks, chunk, rank), jnp.int16),
            pltpu.VMEM((rounds - 1, chunks, 1, rank), jnp.float32),
            pltpu.SemaphoreType.DMA((2,)),
            pltpu.SemaphoreType.DMA((rounds - 1, chunks, 2)),
            pltpu.SemaphoreType.DMA((rounds - 1, chunks, 2)),
        ],
        cost_estimate=pl.CostEstimate(
            flops=18 * n_users * n_items * rank * rounds, bytes_accessed=12 << 20, transcendentals=0
        ),
        compiler_params=pltpu.CompilerParams(
            vmem_limit_bytes=48 << 20, collective_id=0, has_side_effects=True
        ),
        name="sgd_rounds",
    )(items, users, view)


def project(item_content, projection):
    def dot(rows, weights):
        return jnp.dot(rows, weights, preferred_element_type=jnp.float32)

    if lax.axis_size("cat") != 2:
        rows = lax.all_to_all(item_content, "cat", split_axis=0, concat_axis=1, tiled=True)
        return dot(rows, projection)
    me = lax.axis_index("cat")
    rows, width = item_content.shape[0] // 2, item_content.shape[1]
    other = 1 - me
    theirs = lax.dynamic_slice_in_dim(item_content, other * rows, rows)
    got = lax.ppermute(theirs, "cat", [(0, 1), (1, 0)])
    mine = lax.dynamic_slice_in_dim(item_content, me * rows, rows)
    near = dot(mine, lax.dynamic_slice_in_dim(projection, me * width, width))
    return near + dot(got, lax.dynamic_slice_in_dim(projection, other * width, width))


def body(item_content, projection, send_order, user_factors, ratings):
    size = lax.axis_size("blk")
    owned = project(item_content, projection)
    ordered = owned.at[send_order[0]].get(mode="promise_in_bounds")
    dealt = ordered.reshape(size, -1, ordered.shape[1])
    share = dealt.shape[1]
    code = code_of(jnp.max(jnp.abs(dealt), axis=1, keepdims=True))
    sent = jnp.concatenate(
        [coded(dealt, step_of(code)), code.astype(jnp.int32).astype(jnp.int16)], axis=1
    )
    got = lax.all_to_all(sent, "blk", split_axis=0, concat_axis=0, tiled=True)
    got = got.astype(jnp.int32).astype(jnp.float32)
    items = (got[:, :share] * step_of(got[:, share:])).reshape(owned.shape)
    return tuple(all_rounds(items, user_factors, ratings))


def solution(mesh):
    placed = (
        P("blk", "cat"),
        P(),
        P(("blk", "cat"), None),
        P(("blk", "cat"), None),
        P(("blk", "cat"), None, None),
    )
    return jax.shard_map(
        body,
        mesh=mesh,
        in_specs=placed,
        out_specs=(P(("blk", "cat"), None), P(("blk", "cat"), None)),
        check_vma=False,
    )
```

time: 84.9 us -> 75.4 us (0.89)
  blocking collectives: 0 us -> 23.2 us
  waiting for transfers between devices: 32.3 us -> 10.7 us
  starting transfers between devices: 10.4 us -> 3.06 us
  Pallas kernels: 30.8 us -> 27.9 us
  other arithmetic: 2.53 us -> 0.67 us
  local copies, waits for them, and re-layouts: 6.09 us -> 7.38 us
    all_to_all x0 -> x1, blocking collectives: none -> 23.2 us  [body(): got = lax.all_to_all(sent, 'blk', split_axis=0, concat_axis=0, tiled=True)]
    ppermute x6 -> x0, waiting for transfers between devices: 19 us -> none  [body(): sent.append(lax.ppermute(moved, 'blk', ring) if t < rounds - 1 else moved)]
    all_to_all x1 -> x0, starting transfers between devices: 6.13 us -> none  [body(): got = lax.all_to_all(sent, 'blk', split_axis=0, concat_axis=0, tiled=True)]
    pallas_call x9 -> x1, Pallas kernels: 30.8 us -> 27.9 us  [all_rounds(): pl.pallas_call(functools.partial(rounds_kernel, rounds), in_specs=[pl.Blo...]
    all_to_all x1 -> x0, waiting for transfers between devices: 2.63 us -> none  [body(): got = lax.all_to_all(sent, 'blk', split_axis=0, concat_axis=0, tiled=True)]
    unnamed x17 -> x11, local copies, waits for them, and re-layouts: 2.48 us -> 3.87 us
    ppermute x6 -> x0, starting transfers between devices: 1.25 us -> none  [body(): sent.append(lax.ppermute(moved, 'blk', ring) if t < rounds - 1 else moved)]
    concatenate x1 -> x0, other arithmetic: 1.04 us -> none  [body(): return (users, jnp.concatenate(parts))]
  transfers between devices with their start and end apart: 8 -> 1, of which waited for: 8 -> 1; matrix products, arithmetic and copies ran while one was open for 1% -> 2% of each run, Pallas kernels for 30% -> 0%
where the time goes in v1:
time: 75.4 us; the launch traced here: 75.1 us
  Pallas kernels  27.9 us (37%)
  blocking collectives  23.2 us (31%)
  waiting for transfers between devices  10.7 us (14%)
  local copies, waits for them, and re-layouts  7.38 us (10%)
  starting transfers between devices  3.06 us (4%)
  matrix products  1.5 us (2%)
  between operations  0.77 us (1%)
    pallas_call x1, Pallas kernels, all_rounds(): pl.pallas_call(functools.partial(rounds_kernel, rounds), in_specs=[pl.Blo...  27.9 us
    all_to_all x1, blocking collectives, body(): got = lax.all_to_all(sent, 'blk', split_axis=0, concat_axis=0, tiled=True)  23.2 us
    ppermute x1, waiting for transfers between devices, project(): got = lax.ppermute(theirs, 'cat', [(0, 1), (1, 0)])  10.7 us
    unnamed x11, local copies, waits for them, and re-layouts  3.87 us
    gather x1, local copies, waits for them, and re-layouts, body(): ordered = owned.at[send_order[0]].get(mode='promise_in_bounds')  3.47 us
    ppermute x1, starting transfers between devices, project(): got = lax.ppermute(theirs, 'cat', [(0, 1), (1, 0)])  3.06 us
  transfers between devices with their start and end apart: 1, of which 1 were waited for; matrix products, arithmetic and copies ran while one was open for 2% of the time, Pallas kernels for 0%

profile of v1, /device:TPU:0, one launch (start us, length us, event | category | flops | bytes accessed | tf_op | source)
XLA Modules:
  0.0 75.1 jit_solution(6700381561014215574)
XLA Ops:
  0.6 0.0 copy-start
  0.6 1.2 %copy-done = bf16[2048,256]{1,0:T(8,128)(2,1)S(1)} copy-done((bf16[2048,256]{1,0:T(8,128)(2,1)S(1)}, bf16[2048,256]{1,0:T(8,128)(2,1)}, u32[]{:S(2)}) %copy-start) | copy-done | bytes 1048600
  1.9 0.0 copy-start.3
  1.9 0.0 copy-start.2
  1.9 3.1 %collective-permute-start = (bf16[1024,256]{1,0:T(8,128)(2,1)S(1)}, bf16[1024,256]{1,0:T(8,128)(2,1)S(1)}, u32[]{:S(2)}, u32[]{:S(2)}) collective-permute-start(bf16[1024,256]{1,0:T(8,128)(2,1)S(1)} %constant_dynamic-slice_fusion), channel_id=1, source_target_pairs={{0,1},{1,0},{2,3},{3,2},{4,5},{5,4},{6,7},{7,6},{8,9},{9,8},{10,11... | collective-permute-start | bytes 1572872 | tf_op jit(solution)/shard_map/ppermute | solution.py:177
  5.0 1.2 %fusion = f32[1024,256]{1,0:T(8,128)S(1)} fusion(bf16[2048,256]{1,0:T(8,128)(2,1)S(1)} %copy-done, s32[]{:T(128)S(6)} %select_n.22, bf16[512,256]{1,0:T(8,128)(2,1)} %param.6, s32[]{:T(128)S(6)} %select_n.23), kind=kOutput, calls=%fused_computation.7 | convolution fusion | flops 134217728 | bytes 1703944 | tf_op jit(solution)/shard_map/dot_general | solution.py:168
  6.2 0.0 copy-done.3
  6.2 10.7 %collective-permute-done = bf16[1024,256]{1,0:T(8,128)(2,1)S(1)} collective-permute-done((bf16[1024,256]{1,0:T(8,128)(2,1)S(1)}, bf16[1024,256]{1,0:T(8,128)(2,1)S(1)}, u32[]{:S(2)}, u32[]{:S(2)}) %collective-permute-start) | collective-permute-done | bytes 524320 | tf_op jit(solution)/shard_map/ppermute | solution.py:177
  16.9 0.0 copy-done.2
  16.9 0.3 convolution_add_fusion
  17.2 3.5 %gather_fusion = f32[1024,256]{1,0:T(8,128)S(1)} fusion(f32[1024,256]{1,0:T(8,128)S(1)} %convolution_add_fusion, s32[1024]{0:T(1024)S(1)} %broadcast_clamp_fusion), kind=kCustom, calls=%fused_computation | custom fusion | bytes 2101248 | tf_op jit(solution)/shard_map/gather | solution.py:186
  20.7 0.1 abs_reduce_fusion
  20.8 0.2 convert_convert_fusion.1
  21.1 23.2 %all_to_all.5 = s16[16,65,256]{2,1,0:T(8,128)(2,1)S(1)} all-to-all(s16[16,65,256]{2,1,0:T(8,128)(2,1)S(1)} %pad_add_fusion), channel_id=1, replica_groups=mesh['blk'=16,'cat'=2] {'blk'}, dimensions={0} | all-to-all | bytes 1064960 | tf_op jit(solution)/shard_map/all_to_all | solution.py:193
  44.2 0.2 convert_convert_fusion
  44.4 0.0 copy-start.1
  44.5 0.1 slice_multiply_fusion
  44.6 0.9 %copy-done.1 = f32[512,256]{1,0:T(8,128)S(1)} copy-done((f32[512,256]{1,0:T(8,128)S(1)}, f32[512,256]{1,0:T(8,128)}, u32[]{:S(2)}) %copy-start.1) | copy-done | bytes 524312
  45.5 27.9 %sgd_rounds.1 = (f32[512,256]{1,0:T(8,128)S(1)}, f32[1024,256]{1,0:T(8,128)S(1)}) custom-call(f32[1024,256]{1,0:T(8,128)S(1)} %bitcast.18, f32[512,256]{1,0:T(8,128)S(1)} %copy-done.1, s32[16384,128]{1,0:T(8,128)} %bitcast.21), custom_call_target="tpu_custom_call" | custom-call | flops 9663676416 | bytes 12582912 | tf_op jit(solution)/shard_map/sgd_rounds/pallas_call | solution.py:133
  73.4 0.8 %copy.15 = f32[512,256]{1,0:T(8,128)} copy(f32[512,256]{1,0:T(8,128)S(1)} %get-tuple-element.6) | data formatting | bytes 1048576
  74.2 1.0 %copy.16 = f32[1024,256]{1,0:T(8,128)} copy(f32[1024,256]{1,0:T(8,128)S(1)} %get-tuple-element.7) | data formatting | bytes 2097152
  (8 shorter events, 0.2 us)
Async XLA Ops:
  0.6 1.2 %copy-start = (bf16[2048,256]{1,0:T(8,128)(2,1)S(1)}, bf16[2048,256]{1,0:T(8,128)(2,1)}, u32[]{:S(2)}) copy-start(bf16[2048,256]{1,0:T(8,128)(2,1)} %param.5) | copy-start | bytes 3145732
  1.9 4.3 %copy-start.3 = (s32[1,1024]{1,0:T(1,128)S(1)}, s32[1,1024]{1,0:T(1,128)}, u32[]{:S(2)}) copy-start(s32[1,1024]{1,0:T(1,128)} %param.7) | copy-start | bytes 12292
  1.9 15.0 %copy-start.2 = (bf16[512,256]{1,0:T(8,128)(2,1)S(1)}, bf16[512,256]{1,0:T(8,128)(2,1)}, u32[]{:S(2)}) copy-start(bf16[512,256]{1,0:T(8,128)(2,1)} %param.6) | copy-start | bytes 786436
  1.9 15.0 %collective-permute-start = (bf16[1024,256]{1,0:T(8,128)(2,1)S(1)}, bf16[1024,256]{1,0:T(8,128)(2,1)S(1)}, u32[]{:S(2)}, u32[]{:S(2)}) collective-permute-start(bf16[1024,256]{1,0:T(8,128)(2,1)S(1)} %constant_dynamic-slice_fusion), channel_id=1, source_target_pairs={{0,1},{1,0},{2,3},{3,2},{4,5},{5,4},{6,7},{7,6},{8,9},{9,8},{10,11... | collective-permute-start | bytes 1572872 | tf_op jit(solution)/shard_map/ppermute | solution.py:177
  44.4 1.0 %copy-start.1 = (f32[512,256]{1,0:T(8,128)S(1)}, f32[512,256]{1,0:T(8,128)}, u32[]{:S(2)}) copy-start(f32[512,256]{1,0:T(8,128)} %users_in.1) | copy-start | bytes 1572868

commit v2 on v1

v2 whole, which is shorter than its diff:
```python
import functools
import jax
import jax.numpy as jnp
from jax import lax
from jax.experimental import pallas as pl
from jax.experimental.pallas import tpu as pltpu
from jax.sharding import PartitionSpec as P

learn_rate = 0.004
shrink = 0.05
LEVELS = 32000.0
CHUNK = 256
FRONT = 128
LANES = 128
MESH = pl.DeviceIdType.MESH


def split(value):
    high = value.astype(jnp.bfloat16)
    return high, (value - high.astype(jnp.float32)).astype(jnp.bfloat16)


def dot(left, right, dims=((1,), (0,))):
    return lax.dot_general(left, right, (dims, ((), ())), preferred_element_type=jnp.float32)


def product(left, right, dims):
    return dot(left[0], right[0], dims) + (dot(left[0], right[1], dims) + dot(left[1], right[0], dims))


def steps_of(value, axis):
    return jnp.maximum(jnp.max(jnp.abs(value), axis=axis, keepdims=True), 1e-30) * (1.0 / LEVELS)


def coded(value, step):
    return jnp.floor(value * (1.0 / step) + 0.5).astype(jnp.int32).astype(jnp.int16)


def decoded(value, step):
    return value.astype(jnp.int32).astype(jnp.float32) * step


def paired(index, turn, count):
    if count & (count - 1):
        return lax.rem(turn - index + count, count)
    result, bit = index, 1
    while bit < count:
        if turn & bit:
            result = result + bit * (1 - 2 * lax.rem(lax.div(index, bit), 2))
        bit *= 2
    return result


def far_first(count):
    half = count // 2
    return list(range(half, count)) + list(range(half - 1, -1, -1))


def kernel(
    rounds, content_in, weights_in, order_in, users_in, ratings_in, users_out, items_out,
    content, weights, orders, column, near, far_sent, far_got,
    deal_sent, deal_steps, dealt, dealt_steps,
    users, ratings, sent, sent_steps, got, got_steps,
    load_sem, order_send, order_recv, far_send, far_recv, deal_send, deal_recv, send_sem, recv_sem,
):
    size, cats = lax.axis_size("blk"), lax.axis_size("cat")
    me, cat = lax.axis_index("blk"), lax.axis_index("cat")
    n_users, rank = users.shape
    n_items, width = content.shape[1:]
    share = n_items // size
    loads = [
        pltpu.make_async_copy(src, dst, load_sem.at[k])
        for k, (src, dst) in enumerate(
            [
                (order_in, orders.at[0]),
                (content_in, content),
                (weights_in, weights),
                (users_in, users),
                (ratings_in, ratings),
            ]
        )
    ]
    for load in loads:
        load.start()
    barrier = pltpu.get_barrier_semaphore()
    for k in range(1, cats):
        pl.semaphore_signal(barrier, inc=1, device_id={"cat": lax.rem(cat + k, cats)}, device_id_type=MESH)

    def greet(k, carry):
        pl.semaphore_signal(barrier, inc=1, device_id={"blk": lax.rem(me + k, size)}, device_id_type=MESH)
        return carry

    lax.fori_loop(1, size, greet, 0)

    front = far_sent.shape[2]
    fronts = n_items // front
    strata = front // share
    turns = far_first(fronts)

    def spread(slot):
        row = orders[slot].astype(jnp.float32)
        column[slot] = jnp.transpose(jnp.broadcast_to(row, (LANES, n_items)))

    def picked(slot, block, group):
        at = column[slot, pl.ds(pl.multiple_of(group * front, front), front), :]
        lane = lax.broadcasted_iota(jnp.int32, (front, LANES), 1).astype(jnp.float32)
        hot = jnp.concatenate(
            [jnp.where(at == lane + float(j * LANES), 1.0, 0.0).astype(jnp.bfloat16) for j in range(n_items // LANES)],
            axis=1,
        )
        return dot(hot, content[block]).astype(jnp.bfloat16)

    def near_part(n):
        group = paired(lax.div(me, strata), turns[n], fronts)
        near[n] = dot(picked(0, cat, group), weights[cat])

    loads[0].wait()
    spread(0)
    loads[1].wait()
    loads[2].wait()
    for n in range(fronts // 2):
        near_part(n)
    pl.semaphore_wait(barrier, size - 1 + cats - 1)

    def order_move(k):
        return pltpu.make_async_remote_copy(
            src_ref=order_in,
            dst_ref=orders.at[k],
            send_sem=order_send.at[k - 1],
            recv_sem=order_recv.at[k - 1],
            device_id={"cat": lax.rem(cat + k, cats)},
            device_id_type=MESH,
        )

    def far_move(k, n):
        return pltpu.make_async_remote_copy(
            src_ref=far_sent.at[k - 1, n],
            dst_ref=far_got.at[k - 1, n],
            send_sem=far_send.at[k - 1, n],
            recv_sem=far_recv.at[k - 1, n],
            device_id={"cat": lax.rem(cat + k, cats)},
            device_id_type=MESH,
        )

    def deal_moves(stratum, source, target):
        return [
            pltpu.make_async_remote_copy(
                src_ref=src.at[stratum],
                dst_ref=dst.at[source],
                send_sem=deal_send.at[stratum, k],
                recv_sem=deal_recv.at[source, k],
                device_id={"blk": target},
                device_id_type=MESH,
            )
            for k, (src, dst) in enumerate([(deal_sent, dealt), (deal_steps, dealt_steps)])
        ]

    for k in range(1, cats):
        order_move(k).start()
    for n in range(fronts // 2, fronts):
        near_part(n)
    for k in range(1, cats):
        order_move(cats - k).wait_recv()
        spread(cats - k)
        block = lax.rem(cat + k, cats)
        for n in range(fronts):
            group = paired(lax.div(me, strata), turns[n], fronts)
            far_sent[k - 1, n] = picked(cats - k, block, group)
            far_move(k, n).start()
    for n in range(fronts):
        group = paired(lax.div(me, strata), turns[n], fronts)
        owned = near[n]
        for k in range(1, cats):
            far_move(k, n).wait_recv()
            owned += dot(far_got[k - 1, n], weights[lax.rem(cat + cats - k, cats)])
        owned = owned.reshape(strata, share, rank)
        step = steps_of(owned, 1)
        codes = coded(owned, step)
        first = group * strata
        if turns[n] and fronts & (fronts - 1) == 0:
            deal_sent[pl.ds(first, strata)] = codes
            deal_steps[pl.ds(first, strata)] = step
            for i in range(strata):
                for move in deal_moves(first + i, me, first + i):
                    move.start()
        else:
            for i in range(strata):
                stratum = first + i

                @pl.when(stratum == me)
                def _():
                    dealt[me] = codes[i]
                    dealt_steps[me] = step[i]

                @pl.when(stratum != me)
                def _():
                    deal_sent[stratum] = codes[i]
                    deal_steps[stratum] = step[i]
                    for move in deal_moves(stratum, me, stratum):
                        move.start()

    right = lax.rem(me + 1, size)
    chunk = got.shape[2]
    chunks = n_items // chunk
    per = chunk // share
    order = far_first(chunks)
    tiles = n_items // LANES

    def moves(t, n):
        return [
            pltpu.make_async_remote_copy(
                src_ref=src.at[t, n],
                dst_ref=dst.at[t, n],
                send_sem=send_sem.at[t, n, k],
                recv_sem=recv_sem.at[t, n, k],
                device_id={"blk": right},
                device_id_type=MESH,
            )
            for k, (src, dst) in enumerate([(sent, got), (sent_steps, got_steps)])
        ]

    loads[3].wait()
    loads[4].wait()
    for t in range(rounds):
        now = users[...]
        user_parts = split(now)
        user_grad = jnp.zeros(now.shape, jnp.float32)
        start = lax.rem(me - t + size, size)
        for n in range(chunks):
            place = paired(lax.div(start, per), order[n], chunks)
            if t == 0:
                for i in range(per):
                    source = place * per + i

                    @pl.when(source != me)
                    def _():
                        for move in deal_moves(source, source, source):
                            move.wait_recv()

                here = pl.ds(place * per, per)
                old = decoded(dealt[here], dealt_steps[here]).reshape(chunk, rank)
            else:
                for move in moves(t - 1, n):
                    move.wait_recv()
                old = decoded(got[t - 1, n], got_steps[t - 1, n])
            old_parts = split(old)
            guess = product(user_parts, old_parts, ((1,), (1,)))
            first = place * (chunk // LANES)
            values = jnp.concatenate(
                [
                    ratings[pl.ds((first + j) * rounds + t, n_users, stride=tiles * rounds), :]
                    for j in range(chunk // LANES)
                ],
                axis=1,
            ).astype(jnp.float32)
            errors = jnp.where(values > 0.0, values - guess, 0.0)
            error_parts = split(errors)
            item_grad = product(error_parts, user_parts, ((0,), (0,)))
            new = old + learn_rate * (item_grad - shrink * old)
            if t < rounds - 1:
                step = steps_of(new, 0)
                sent[t, n] = coded(new, step)
                sent_steps[t, n] = step
                for move in moves(t, n):
                    move.start()
            else:
                items_out[pl.ds(pl.multiple_of(place * chunk, chunk), chunk), :] = new
            user_grad += product(error_parts, old_parts, ((1,), (0,)))
        now = now + learn_rate * (user_grad - shrink * now)
        if t < rounds - 1:
            users[...] = now
        else:
            users_out[...] = now

    for k in range(1, cats):
        order_move(k).wait_send()
        for n in range(fronts):
            far_move(k, n).wait_send()

    def settle(stratum, carry):
        @pl.when(stratum != me)
        def _():
            for move in deal_moves(stratum, me, stratum):
                move.wait_send()

        return carry

    lax.fori_loop(0, size, settle, 0)
    for t in range(rounds - 1):
        for n in range(chunks):
            for move in moves(t, n):
                move.wait_send()


def body(item_content, projection, send_order, user_factors, ratings):
    size, cats = lax.axis_size("blk"), lax.axis_size("cat")
    n_users, rounds, n_items = ratings.shape
    width, rank = item_content.shape[1], user_factors.shape[1]
    share = n_items // size
    chunk, front = max(CHUNK, share), max(FRONT, share)
    chunks, fronts = n_items // chunk, n_items // front
    view = ratings.reshape(n_users, rounds, n_items // LANES, LANES).transpose(0, 2, 1, 3).reshape(-1, LANES)
    dma = pltpu.SemaphoreType.DMA
    return tuple(
        pl.pallas_call(
            functools.partial(kernel, rounds),
            in_specs=[pl.BlockSpec(memory_space=pl.ANY)] * 5,
            out_specs=[pl.BlockSpec(memory_space=pltpu.VMEM)] * 2,
            out_shape=[
                jax.ShapeDtypeStruct((n_users, rank), jnp.float32),
                jax.ShapeDtypeStruct((n_items, rank), jnp.float32),
            ],
            scratch_shapes=[
                pltpu.VMEM((cats, n_items, width), jnp.bfloat16),
                pltpu.VMEM((cats, width, rank), jnp.bfloat16),
                pltpu.VMEM((cats, 1, n_items), jnp.int32),
                pltpu.VMEM((cats, n_items, LANES), jnp.float32),
                pltpu.VMEM((fronts, front, rank), jnp.float32),
                pltpu.VMEM((cats - 1, fronts, front, width), jnp.bfloat16),
                pltpu.VMEM((cats - 1, fronts, front, width), jnp.bfloat16),
                pltpu.VMEM((size, share, rank), jnp.int16),
                pltpu.VMEM((size, 1, rank), jnp.float32),
                pltpu.VMEM((size, share, rank), jnp.int16),
                pltpu.VMEM((size, 1, rank), jnp.float32),
                pltpu.VMEM((n_users, rank), jnp.float32),
                pltpu.VMEM(view.shape, jnp.int32),
                pltpu.VMEM((rounds - 1, chunks, chunk, rank), jnp.int16),
                pltpu.VMEM((rounds - 1, chunks, 1, rank), jnp.float32),
                pltpu.VMEM((rounds - 1, chunks, chunk, rank), jnp.int16),
                pltpu.VMEM((rounds - 1, chunks, 1, rank), jnp.float32),
                dma((5,)),
                dma((cats - 1,)),
                dma((cats - 1,)),
                dma((cats - 1, fronts)),
                dma((cats - 1, fronts)),
                dma((size, 2)),
                dma((size, 2)),
                dma((rounds - 1, chunks, 2)),
                dma((rounds - 1, chunks, 2)),
            ],
            cost_estimate=pl.CostEstimate(
                flops=18 * n_users * n_items * rank * rounds, bytes_accessed=12 << 20, transcendentals=0
            ),
            compiler_params=pltpu.CompilerParams(
                vmem_limit_bytes=48 << 20, collective_id=0, has_side_effects=True
            ),
            name="stratified_sgd",
        )(
            item_content.reshape(cats, n_items, width),
            projection.reshape(cats, width, rank),
            send_order,
            user_factors,
            view,
        )
    )


def solution(mesh):
    placed = (
        P("blk", "cat"),
        P(),
        P(("blk", "cat"), None),
        P(("blk", "cat"), None),
        P(("blk", "cat"), None, None),
    )
    return jax.shard_map(
        body,
        mesh=mesh,
        in_specs=placed,
        out_specs=(P(("blk", "cat"), None), P(("blk", "cat"), None)),
        check_vma=False,
    )
```

time: 75.4 us -> 56.2 us (0.75)
  blocking collectives: 23.2 us -> 0 us
  Pallas kernels: 27.9 us -> 49.6 us
  waiting for transfers between devices: 10.7 us -> 0 us
  starting transfers between devices: 3.06 us -> 0 us
  local copies, waits for them, and re-layouts: 7.38 us -> 5.66 us
  matrix products: 1.5 us -> 0 us
    all_to_all x1 -> x0, blocking collectives: 23.2 us -> none  [body(): got = lax.all_to_all(sent, 'blk', split_axis=0, concat_axis=0, tiled=True)]
    pallas_call x1, Pallas kernels: 27.9 us -> 49.6 us  [body(): pl.pallas_call(functools.partial(kernel, rounds), in_specs=[pl.BlockSpec(...]
    ppermute x1 -> x0, waiting for transfers between devices: 10.7 us -> none  [project(): got = lax.ppermute(theirs, 'cat', [(0, 1), (1, 0)])]
    gather x1 -> x0, local copies, waits for them, and re-layouts: 3.47 us -> none  [body(): ordered = owned.at[send_order[0]].get(mode='promise_in_bounds')]
    ppermute x1 -> x0, starting transfers between devices: 3.06 us -> none  [project(): got = lax.ppermute(theirs, 'cat', [(0, 1), (1, 0)])]
    unnamed x11 -> x10, local copies, waits for them, and re-layouts: 3.87 us -> 5.66 us
    dot_general x2 -> x0, matrix products: 1.5 us -> none  [dot(): return jnp.dot(rows, weights, preferred_element_type=jnp.float32)]
  transfers between devices with their start and end apart: 1 -> 0, of which waited for: 1 -> 0; matrix products, arithmetic and copies ran while one was open for 2% -> 0% of each run, Pallas kernels for 0% -> 0%
where the time goes in v2:
time: 56.2 us; the launch traced here: 55.9 us
  Pallas kernels  49.6 us (88%)
  local copies, waits for them, and re-layouts  5.66 us (10%)
  between operations  0.65 us (1%)
    pallas_call x1, Pallas kernels, body(): pl.pallas_call(functools.partial(kernel, rounds), in_specs=[pl.BlockSpec(...  49.6 us
    unnamed x10, local copies, waits for them, and re-layouts  5.66 us

profile of v2, /device:TPU:0, one launch (start us, length us, event | category | flops | bytes accessed | tf_op | source)
XLA Modules:
  0.0 55.9 jit_solution(13023207556262616593)
XLA Ops:
  0.6 0.0 copy-start
  0.6 1.2 %copy-done = bf16[2048,256]{1,0:T(8,128)(2,1)S(1)} copy-done((bf16[2048,256]{1,0:T(8,128)(2,1)S(1)}, bf16[2048,256]{1,0:T(8,128)(2,1)}, u32[]{:S(2)}) %copy-start) | copy-done | bytes 1048600
  1.9 0.0 copy-start.1
  1.9 1.0 %copy-done.1 = f32[512,256]{1,0:T(8,128)S(1)} copy-done((f32[512,256]{1,0:T(8,128)S(1)}, f32[512,256]{1,0:T(8,128)}, u32[]{:S(2)}) %copy-start.1) | copy-done | bytes 524312
  2.9 0.0 copy-start.2
  2.9 0.9 %copy-done.2 = bf16[512,256]{1,0:T(8,128)(2,1)S(1)} copy-done((bf16[512,256]{1,0:T(8,128)(2,1)S(1)}, bf16[512,256]{1,0:T(8,128)(2,1)}, u32[]{:S(2)}) %copy-start.2) | copy-done | bytes 262168
  3.8 0.0 copy-start.3
  3.9 0.7 %copy-done.3 = s32[1,1024]{1,0:T(1,128)S(1)} copy-done((s32[1,1024]{1,0:T(1,128)S(1)}, s32[1,1024]{1,0:T(1,128)}, u32[]{:S(2)}) %copy-start.3) | copy-done | bytes 4120
  4.5 49.6 %stratified_sgd.1 = (f32[512,256]{1,0:T(8,128)S(1)}, f32[1024,256]{1,0:T(8,128)S(1)}) custom-call(bf16[2,1024,256]{2,1,0:T(8,128)(2,1)S(1)} %bitcast.7, bf16[2,256,256]{2,1,0:T(8,128)(2,1)S(1)} %bitcast.8, s32[1,1024]{1,0:T(1,128)S(1)} %copy-done.3, f32[512,256]{1,0:T(8,128)S(1)} %copy-done.1, s32[16384,128]{1,0:T(8,128)} %bitcast.9), custom_call_target="tpu_custom_call" | custom-call | flops 9663676416 | bytes 12582912 | tf_op jit(solution)/shard_map/stratified_sgd/pallas_call | solution.py:305
  54.2 0.8 %copy.10 = f32[512,256]{1,0:T(8,128)} copy(f32[512,256]{1,0:T(8,128)S(1)} %get-tuple-element.4) | data formatting | bytes 1048576
  55.0 1.0 %copy.11 = f32[1024,256]{1,0:T(8,128)} copy(f32[1024,256]{1,0:T(8,128)S(1)} %get-tuple-element.5) | data formatting | bytes 2097152
Async XLA Ops:
  0.6 1.2 %copy-start = (bf16[2048,256]{1,0:T(8,128)(2,1)S(1)}, bf16[2048,256]{1,0:T(8,128)(2,1)}, u32[]{:S(2)}) copy-start(bf16[2048,256]{1,0:T(8,128)(2,1)} %param.5) | copy-start | bytes 3145732
  1.9 1.0 %copy-start.1 = (f32[512,256]{1,0:T(8,128)S(1)}, f32[512,256]{1,0:T(8,128)}, u32[]{:S(2)}) copy-start(f32[512,256]{1,0:T(8,128)} %users_in.1) | copy-start | bytes 1572868
  2.9 0.9 %copy-start.2 = (bf16[512,256]{1,0:T(8,128)(2,1)S(1)}, bf16[512,256]{1,0:T(8,128)(2,1)}, u32[]{:S(2)}) copy-start(bf16[512,256]{1,0:T(8,128)(2,1)} %param.6) | copy-start | bytes 786436
  3.8 0.7 %copy-start.3 = (s32[1,1024]{1,0:T(1,128)S(1)}, s32[1,1024]{1,0:T(1,128)}, u32[]{:S(2)}) copy-start(s32[1,1024]{1,0:T(1,128)} %order_in.1) | copy-start | bytes 12292

commit v3 on v2

--- a/solution.py
+++ b/solution.py
@@ -56,11 +56,19 @@
     return list(range(half, count)) + list(range(half - 1, -1, -1))
 
 
+def near_first(count):
+    return [count // 2] + list(range(count // 2 - 1, -1, -1)) + list(range(count // 2 + 1, count))
+
+
+def unpacked_early(count):
+    return count // 4
+
+
 def kernel(
     rounds, content_in, weights_in, order_in, users_in, ratings_in, users_out, items_out,
     content, weights, orders, column, near, far_sent, far_got,
     deal_sent, deal_steps, dealt, dealt_steps,
-    users, ratings, sent, sent_steps, got, got_steps,
+    users, ratings, values, sent, sent_steps, got, got_steps,
     load_sem, order_send, order_recv, far_send, far_recv, deal_send, deal_recv, send_sem, recv_sem,
 ):
     size, cats = lax.axis_size("blk"), lax.axis_size("cat")
@@ -167,7 +175,7 @@
             group = paired(lax.div(me, strata), turns[n], fronts)
             far_sent[k - 1, n] = picked(cats - k, block, group)
             far_move(k, n).start()
-    for n in range(fronts):
+    def deal(n):
         group = paired(lax.div(me, strata), turns[n], fronts)
         owned = near[n]
         for k in range(1, cats):
@@ -203,7 +211,7 @@
     chunk = got.shape[2]
     chunks = n_items // chunk
     per = chunk // share
-    order = far_first(chunks)
+    order = near_first(chunks)
     tiles = n_items // LANES
 
     def moves(t, n):
@@ -219,58 +227,87 @@
             for k, (src, dst) in enumerate([(sent, got), (sent_steps, got_steps)])
         ]
 
+    def unpack(piece):
+        t, n = divmod(piece, chunks)
+        for j in range(chunk // LANES):
+            tile = n * (chunk // LANES) + j
+            part = ratings[pl.ds(tile * rounds + t, n_users, stride=tiles * rounds), :]
+            values[t, n, :, pl.ds(j * LANES, LANES)] = part.astype(jnp.float32).astype(jnp.bfloat16)
+
+    def round_step(t, n, user_parts, kept, grads):
+        place = paired(lax.div(lax.rem(me - t + size, size), per), order[n], chunks)
+        if t == 0:
+            for i in range(per):
+                source = place * per + i
+
+                @pl.when(source != me)
+                def _():
+                    for move in deal_moves(source, source, source):
+                        move.wait_recv()
+
+            here = pl.ds(place * per, per)
+            old = decoded(dealt[here], dealt_steps[here]).reshape(chunk, rank)
+        else:
+            for move in moves(t - 1, n):
+                move.wait_recv()
+            old = decoded(got[t - 1, n], got_steps[t - 1, n])
+        old_parts = split(old)
+        guess = product(user_parts, old_parts, ((1,), (1,)))
+        rated = values[t, place].astype(jnp.float32)
+        error_parts = split(jnp.where(rated > 0.0, rated - guess, 0.0))
+        if kept:
+            grads.append(product(*kept.pop(), ((1,), (0,))))
+        item_grad = product(error_parts, user_parts, ((0,), (0,)))
+        new = old + learn_rate * (item_grad - shrink * old)
+        if t < rounds - 1:
+            step = steps_of(new, 0)
+            sent[t, n] = coded(new, step)
+            sent_steps[t, n] = step
+        else:
+            items_out[pl.ds(pl.multiple_of(place * chunk, chunk), chunk), :] = new
+        if n < chunks - 1:
+            kept.append((error_parts, old_parts))
+        else:
+            grads.append(product(error_parts, old_parts, ((1,), (0,))))
+        if t < rounds - 1:
+            for move in moves(t, n):
+                move.start()
+
     loads[3].wait()
     loads[4].wait()
+    pieces = list(range(rounds * chunks))
+
+    def unpack_some(count):
+        for piece in pieces[:count]:
+            unpack(piece)
+        del pieces[:count]
+
+    early = unpacked_early(rounds * chunks)
+    unpack_some(early)
+    each = pl.cdiv(len(pieces), fronts)
+    parts = fronts // chunks
+    now = users[...]
+    user_parts = split(now)
+    kept, grads = [], []
+
+    def first_round(n):
+        round_step(0, n, user_parts, kept, grads)
+
+    for n in range(fronts):
+        deal(n)
+        unpack_some(each)
+        if n == fronts - 1 - parts:
+            first_round(0)
+    unpack_some(len(pieces))
+    for n in range(1, chunks):
+        first_round(n)
     for t in range(rounds):
-        now = users[...]
-        user_parts = split(now)
-        user_grad = jnp.zeros(now.shape, jnp.float32)
-        start = lax.rem(me - t + size, size)
-        for n in range(chunks):
-            place = paired(lax.div(start, per), order[n], chunks)
-            if t == 0:
-                for i in range(per):
-                    source = place * per + i
-
-                    @pl.when(source != me)
-                    def _():
-                        for move in deal_moves(source, source, source):
-                            move.wait_recv()
-
-                here = pl.ds(place * per, per)
-                old = decoded(dealt[here], dealt_steps[here]).reshape(chunk, rank)
-            else:
-                for move in moves(t - 1, n):
-                    move.wait_recv()
-                old = decoded(got[t - 1, n], got_steps[t - 1, n])
-            old_parts = split(old)
-            guess = product(user_parts, old_parts, ((1,), (1,)))
-            first = place * (chunk // LANES)
-            values = jnp.concatenate(
-                [
-                    ratings[pl.ds((first + j) * rounds + t, n_users, stride=tiles * rounds), :]
-                    for j in range(chunk // LANES)
-                ],
-                axis=1,
-            ).astype(jnp.float32)
-            errors = jnp.where(values > 0.0, values - guess, 0.0)
-            error_parts = split(errors)
-            item_grad = product(error_parts, user_parts, ((0,), (0,)))
-            new = old + learn_rate * (item_grad - shrink * old)
-            if t < rounds - 1:
-                step = steps_of(new, 0)
-                sent[t, n] = coded(new, step)
-                sent_steps[t, n] = step
-                for move in moves(t, n):
-                    move.start()
-            else:
-                items_out[pl.ds(pl.multiple_of(place * chunk, chunk), chunk), :] = new
-            user_grad += product(error_parts, old_parts, ((1,), (0,)))
-        now = now + learn_rate * (user_grad - shrink * now)
-        if t < rounds - 1:
-            users[...] = now
-        else:
-            users_out[...] = now
+        if t > 0:
+            user_parts, grads = split(now), []
+            for n in range(chunks):
+                round_step(t, n, user_parts, kept, grads)
+        now = now + learn_rate * (functools.reduce(jnp.add, grads) - shrink * now)
+    users_out[...] = now
 
     for k in range(1, cats):
         order_move(k).wait_send()
@@ -324,6 +361,7 @@
                 pltpu.VMEM((size, 1, rank), jnp.float32),
                 pltpu.VMEM((n_users, rank), jnp.float32),
                 pltpu.VMEM(view.shape, jnp.int32),
+                pltpu.VMEM((rounds, chunks, n_users, chunk), jnp.bfloat16),
                 pltpu.VMEM((rounds - 1, chunks, chunk, rank), jnp.int16),
                 pltpu.VMEM((rounds - 1, chunks, 1, rank), jnp.float32),
                 pltpu.VMEM((rounds - 1, chunks, chunk, rank), jnp.int16),
@@ -346,11 +384,16 @@
             ),
             name="stratified_sgd",
         )(
-            item_content.reshape(cats, n_items, width),
-            projection.reshape(cats, width, rank),
-            send_order,
-            user_factors,
-            view,
+            *[
+                pltpu.with_memory_space_constraint(value, pltpu.HBM)
+                for value in (
+                    item_content.reshape(cats, n_items, width),
+                    projection.reshape(cats, width, rank),
+                    send_order,
+                    user_factors,
+                    view,
+                )
+            ]
         )
     )
 

time: 56.2 us -> 54.4 us (0.968)
  local copies, waits for them, and re-layouts: 5.66 us -> 1.77 us
  Pallas kernels: 49.6 us -> 51.8 us
    unnamed x10 -> x2, local copies, waits for them, and re-layouts: 5.66 us -> 1.77 us
    pallas_call x1, Pallas kernels: 49.6 us -> 51.8 us  [body(): pl.pallas_call(functools.partial(kernel, rounds), in_specs=[pl.BlockSpec(...]
where the time goes in v3:
time: 54.4 us; the launch traced here: 54.2 us
  Pallas kernels  51.8 us (95%)
  local copies, waits for them, and re-layouts  1.77 us (3%)
  between operations  0.64 us (1%)
    pallas_call x1, Pallas kernels, body(): pl.pallas_call(functools.partial(kernel, rounds), in_specs=[pl.BlockSpec(...  51.8 us
    unnamed x2, local copies, waits for them, and re-layouts  1.77 us

profile of v3, /device:TPU:0, one launch (start us, length us, event | category | flops | bytes accessed | tf_op | source)
XLA Modules:
  0.0 54.2 jit_solution(1257358383629476853)
XLA Ops:
  0.6 51.8 %stratified_sgd.1 = (f32[512,256]{1,0:T(8,128)S(1)}, f32[1024,256]{1,0:T(8,128)S(1)}) custom-call(bf16[2,1024,256]{2,1,0:T(8,128)(2,1)} %bitcast.8, bf16[2,256,256]{2,1,0:T(8,128)(2,1)} %bitcast.9, s32[1,1024]{1,0:T(1,128)} %order_in.1, f32[512,256]{1,0:T(8,128)} %users_in.1, s32[16384,128]{1,0:T(8,128)} %bitcast.7), custom_call_target="tpu_custom_call" | custom-call | flops 9663676416 | bytes 12582912 | tf_op jit(solution)/shard_map/stratified_sgd/pallas_call | solution.py:342
  52.5 0.8 %copy.10 = f32[512,256]{1,0:T(8,128)} copy(f32[512,256]{1,0:T(8,128)S(1)} %get-tuple-element.4) | data formatting | bytes 1048576
  53.3 1.0 %copy.11 = f32[1024,256]{1,0:T(8,128)} copy(f32[1024,256]{1,0:T(8,128)S(1)} %get-tuple-element.5) | data formatting | bytes 2097152

commit v4 on v3

--- a/solution.py
+++ b/solution.py
@@ -10,7 +10,7 @@
 shrink = 0.05
 LEVELS = 32000.0
 CHUNK = 256
-FRONT = 128
+FRONT = 256
 LANES = 128
 MESH = pl.DeviceIdType.MESH
 
@@ -240,10 +240,14 @@
             for i in range(per):
                 source = place * per + i
 
-                @pl.when(source != me)
-                def _():
+                def arrive():
                     for move in deal_moves(source, source, source):
                         move.wait_recv()
+
+                if order[n] and chunks & (chunks - 1) == 0:
+                    arrive()
+                else:
+                    pl.when(source != me)(arrive)
 
             here = pl.ds(place * per, per)
             old = decoded(dealt[here], dealt_steps[here]).reshape(chunk, rank)
@@ -285,7 +289,6 @@
     early = unpacked_early(rounds * chunks)
     unpack_some(early)
     each = pl.cdiv(len(pieces), fronts)
-    parts = fronts // chunks
     now = users[...]
     user_parts = split(now)
     kept, grads = [], []
@@ -296,10 +299,8 @@
     for n in range(fronts):
         deal(n)
         unpack_some(each)
-        if n == fronts - 1 - parts:
-            first_round(0)
     unpack_some(len(pieces))
-    for n in range(1, chunks):
+    for n in range(chunks):
         first_round(n)
     for t in range(rounds):
         if t > 0:

time: 54.4 us -> 51.7 us (0.950)
  Pallas kernels: 51.8 us -> 49.1 us
    pallas_call x1, Pallas kernels: 51.8 us -> 49.1 us  [body(): pl.pallas_call(functools.partial(kernel, rounds), in_specs=[pl.BlockSpec(...]
where the time goes in v4:
time: 51.7 us; the launch traced here: 51.5 us
  Pallas kernels  49.1 us (95%)
  local copies, waits for them, and re-layouts  1.77 us (3%)
  between operations  0.64 us (1%)
    pallas_call x1, Pallas kernels, body(): pl.pallas_call(functools.partial(kernel, rounds), in_specs=[pl.BlockSpec(...  49.1 us
    unnamed x2, local copies, waits for them, and re-layouts  1.77 us

profile of v4, /device:TPU:0, one launch (start us, length us, event | category | flops | bytes accessed | tf_op | source)
XLA Modules:
  0.0 51.5 jit_solution(3725907974475365618)
XLA Ops:
  0.6 49.1 %stratified_sgd.1 = (f32[512,256]{1,0:T(8,128)S(1)}, f32[1024,256]{1,0:T(8,128)S(1)}) custom-call(bf16[2,1024,256]{2,1,0:T(8,128)(2,1)} %bitcast.8, bf16[2,256,256]{2,1,0:T(8,128)(2,1)} %bitcast.9, s32[1,1024]{1,0:T(1,128)} %order_in.1, f32[512,256]{1,0:T(8,128)} %users_in.1, s32[16384,128]{1,0:T(8,128)} %bitcast.7), custom_call_target="tpu_custom_call" | custom-call | flops 9663676416 | bytes 12582912 | tf_op jit(solution)/shard_map/stratified_sgd/pallas_call | solution.py:343
  49.7 0.8 %copy.10 = f32[512,256]{1,0:T(8,128)} copy(f32[512,256]{1,0:T(8,128)S(1)} %get-tuple-element.4) | data formatting | bytes 1048576
  50.5 1.0 %copy.11 = f32[1024,256]{1,0:T(8,128)} copy(f32[1024,256]{1,0:T(8,128)S(1)} %get-tuple-element.5) | data formatting | bytes 2097152

commit v5 on v4

--- a/solution.py
+++ b/solution.py
@@ -232,7 +232,7 @@
         for j in range(chunk // LANES):
             tile = n * (chunk // LANES) + j
             part = ratings[pl.ds(tile * rounds + t, n_users, stride=tiles * rounds), :]
-            values[t, n, :, pl.ds(j * LANES, LANES)] = part.astype(jnp.float32).astype(jnp.bfloat16)
+            values[t, n, pl.ds(j * LANES, LANES), :] = jnp.transpose(part.astype(jnp.float32)).astype(jnp.bfloat16)
 
     def round_step(t, n, user_parts, kept, grads):
         place = paired(lax.div(lax.rem(me - t + size, size), per), order[n], chunks)
@@ -256,12 +256,12 @@
                 move.wait_recv()
             old = decoded(got[t - 1, n], got_steps[t - 1, n])
         old_parts = split(old)
-        guess = product(user_parts, old_parts, ((1,), (1,)))
+        guess = product(old_parts, user_parts, ((1,), (1,)))
         rated = values[t, place].astype(jnp.float32)
         error_parts = split(jnp.where(rated > 0.0, rated - guess, 0.0))
         if kept:
-            grads.append(product(*kept.pop(), ((1,), (0,))))
-        item_grad = product(error_parts, user_parts, ((0,), (0,)))
+            grads.append(product(*kept.pop(), ((0,), (0,))))
+        item_grad = product(error_parts, user_parts, ((1,), (0,)))
         new = old + learn_rate * (item_grad - shrink * old)
         if t < rounds - 1:
             step = steps_of(new, 0)
@@ -269,13 +269,13 @@
             sent_steps[t, n] = step
         else:
             items_out[pl.ds(pl.multiple_of(place * chunk, chunk), chunk), :] = new
+        if t < rounds - 1:
+            for move in moves(t, n):
+                move.start()
         if n < chunks - 1:
             kept.append((error_parts, old_parts))
         else:
-            grads.append(product(error_parts, old_parts, ((1,), (0,))))
-        if t < rounds - 1:
-            for move in moves(t, n):
-                move.start()
+            grads.append(product(error_parts, old_parts, ((0,), (0,))))
 
     loads[3].wait()
     loads[4].wait()
@@ -330,6 +330,31 @@
                 move.wait_send()
 
 
+def finish(users_in, items_in, users_out, items_out, sem):
+    moves = [
+        pltpu.make_async_copy(users_in, users_out, sem.at[0]),
+        pltpu.make_async_copy(items_in, items_out, sem.at[1]),
+    ]
+    for move in moves:
+        move.start()
+    for move in moves:
+        move.wait()
+
+
+def finished(users, items):
+    return tuple(
+        pl.pallas_call(
+            finish,
+            in_specs=[pl.BlockSpec(memory_space=pltpu.VMEM)] * 2,
+            out_specs=[pl.BlockSpec(memory_space=pltpu.HBM)] * 2,
+            out_shape=[jax.ShapeDtypeStruct(value.shape, value.dtype) for value in (users, items)],
+            scratch_shapes=[pltpu.SemaphoreType.DMA((2,))],
+            compiler_params=pltpu.CompilerParams(vmem_limit_bytes=8 << 20),
+            name="finish",
+        )(users, items)
+    )
+
+
 def body(item_content, projection, send_order, user_factors, ratings):
     size, cats = lax.axis_size("blk"), lax.axis_size("cat")
     n_users, rounds, n_items = ratings.shape
@@ -339,8 +364,8 @@
     chunks, fronts = n_items // chunk, n_items // front
     view = ratings.reshape(n_users, rounds, n_items // LANES, LANES).transpose(0, 2, 1, 3).reshape(-1, LANES)
     dma = pltpu.SemaphoreType.DMA
-    return tuple(
-        pl.pallas_call(
+    return finished(
+        *pl.pallas_call(
             functools.partial(kernel, rounds),
             in_specs=[pl.BlockSpec(memory_space=pl.ANY)] * 5,
             out_specs=[pl.BlockSpec(memory_space=pltpu.VMEM)] * 2,
@@ -362,7 +387,7 @@
                 pltpu.VMEM((size, 1, rank), jnp.float32),
                 pltpu.VMEM((n_users, rank), jnp.float32),
                 pltpu.VMEM(view.shape, jnp.int32),
-                pltpu.VMEM((rounds, chunks, n_users, chunk), jnp.bfloat16),
+                pltpu.VMEM((rounds, chunks, chunk, n_users), jnp.bfloat16),
                 pltpu.VMEM((rounds - 1, chunks, chunk, rank), jnp.int16),
                 pltpu.VMEM((rounds - 1, chunks, 1, rank), jnp.float32),
                 pltpu.VMEM((rounds - 1, chunks, chunk, rank), jnp.int16),

time: 51.7 us -> 51.2 us (level)
  local copies, waits for them, and re-layouts: 1.77 us -> 0 us
  Pallas kernels: 49.1 us -> 50.2 us
    unnamed x2 -> x0, local copies, waits for them, and re-layouts: 1.77 us -> none
    pallas_call x0 -> x1, Pallas kernels: none -> 1.16 us  [finished(): pl.pallas_call(finish, in_specs=[pl.BlockSpec(memory_space=pltpu.VMEM)] *...]
where the time goes in v5:
time: 51.2 us; the launch traced here: 51 us
  Pallas kernels  50.2 us (98%)
  between operations  0.82 us (2%)
    pallas_call x1, Pallas kernels, body(): pl.pallas_call(functools.partial(kernel, rounds), in_specs=[pl.BlockSpec(...  49.1 us
    pallas_call x1, Pallas kernels, finished(): pl.pallas_call(finish, in_specs=[pl.BlockSpec(memory_space=pltpu.VMEM)] *...  1.16 us

profile of v5, /device:TPU:0, one launch (start us, length us, event | category | flops | bytes accessed | tf_op | source)
XLA Modules:
  0.0 51.0 jit_solution(1682599587643643156)
XLA Ops:
  0.6 49.1 %stratified_sgd.1 = (f32[512,256]{1,0:T(8,128)S(1)}, f32[1024,256]{1,0:T(8,128)S(1)}) custom-call(bf16[2,1024,256]{2,1,0:T(8,128)(2,1)} %bitcast.8, bf16[2,256,256]{2,1,0:T(8,128)(2,1)} %bitcast.9, s32[1,1024]{1,0:T(1,128)} %order_in.1, f32[512,256]{1,0:T(8,128)} %users_in.1, s32[16384,128]{1,0:T(8,128)} %bitcast.7), custom_call_target="tpu_custom_call" | custom-call | flops 9663676416 | bytes 12582912 | tf_op jit(solution)/shard_map/stratified_sgd/pallas_call | solution.py:368
  49.7 1.2 %finish.1 = (f32[512,256]{1,0:T(8,128)}, f32[1024,256]{1,0:T(8,128)}) custom-call(f32[512,256]{1,0:T(8,128)S(1)} %get-tuple-element.4.users_in, f32[1024,256]{1,0:T(8,128)S(1)} %get-tuple-element.5.items_in), custom_call_target="tpu_custom_call" | custom-call | tf_op jit(solution)/shard_map/finish/pallas_call | solution.py:346

commit v6 on v5

--- a/solution.py
+++ b/solution.py
@@ -51,13 +51,13 @@
     return result
 
 
-def far_first(count):
-    half = count // 2
-    return list(range(half, count)) + list(range(half - 1, -1, -1))
-
-
-def near_first(count):
-    return [count // 2] + list(range(count // 2 - 1, -1, -1)) + list(range(count // 2 + 1, count))
+def alternate(count):
+    half, turns = count // 2, []
+    for i in range(count - half):
+        turns.append(half + i)
+        if i < half:
+            turns.append(half - 1 - i)
+    return turns
 
 
 def unpacked_early(count):
@@ -103,7 +103,7 @@
     front = far_sent.shape[2]
     fronts = n_items // front
     strata = front // share
-    turns = far_first(fronts)
+    turns = alternate(fronts)
 
     def spread(slot):
         row = orders[slot].astype(jnp.float32)
@@ -211,7 +211,7 @@
     chunk = got.shape[2]
     chunks = n_items // chunk
     per = chunk // share
-    order = near_first(chunks)
+    order = alternate(chunks)
     tiles = n_items // LANES
 
     def moves(t, n):

time: 51.2 us -> 49.2 us (0.961)
  Pallas kernels: 50.2 us -> 48.2 us
    pallas_call x1, Pallas kernels: 49.1 us -> 47.1 us  [body(): pl.pallas_call(functools.partial(kernel, rounds), in_specs=[pl.BlockSpec(...]
where the time goes in v6:
time: 49.2 us; the launch traced here: 49.1 us
  Pallas kernels  48.2 us (98%)
  between operations  0.82 us (2%)
    pallas_call x1, Pallas kernels, body(): pl.pallas_call(functools.partial(kernel, rounds), in_specs=[pl.BlockSpec(...  47.1 us
    pallas_call x1, Pallas kernels, finished(): pl.pallas_call(finish, in_specs=[pl.BlockSpec(memory_space=pltpu.VMEM)] *...  1.16 us

profile of v6, /device:TPU:0, one launch (start us, length us, event | category | flops | bytes accessed | tf_op | source)
XLA Modules:
  0.0 49.1 jit_solution(310707743322474740)
XLA Ops:
  0.6 47.1 %stratified_sgd.1 = (f32[512,256]{1,0:T(8,128)S(1)}, f32[1024,256]{1,0:T(8,128)S(1)}) custom-call(bf16[2,1024,256]{2,1,0:T(8,128)(2,1)} %bitcast.8, bf16[2,256,256]{2,1,0:T(8,128)(2,1)} %bitcast.9, s32[1,1024]{1,0:T(1,128)} %order_in.1, f32[512,256]{1,0:T(8,128)} %users_in.1, s32[16384,128]{1,0:T(8,128)} %bitcast.7), custom_call_target="tpu_custom_call" | custom-call | flops 9663676416 | bytes 12582912 | tf_op jit(solution)/shard_map/stratified_sgd/pallas_call | solution.py:368
  47.7 1.2 %finish.1 = (f32[512,256]{1,0:T(8,128)}, f32[1024,256]{1,0:T(8,128)}) custom-call(f32[512,256]{1,0:T(8,128)S(1)} %get-tuple-element.4.users_in, f32[1024,256]{1,0:T(8,128)S(1)} %get-tuple-element.5.items_in), custom_call_target="tpu_custom_call" | custom-call | tf_op jit(solution)/shard_map/finish/pallas_call | solution.py:346

commit v7 on v6

--- a/solution.py
+++ b/solution.py
@@ -61,7 +61,7 @@
 
 
 def unpacked_early(count):
-    return count // 4
+    return count * 5 // 8
 
 
 def kernel(

time: 49.2 us -> 54.1 us (1.100)
  Pallas kernels: 48.2 us -> 53.1 us
    pallas_call x1, Pallas kernels: 47.1 us -> 51.9 us  [body(): pl.pallas_call(functools.partial(kernel, rounds), in_specs=[pl.BlockSpec(...]
where the time goes in v7:
time: 54.1 us; the launch traced here: 53.9 us
  Pallas kernels  53.1 us (98%)
  between operations  0.8 us (1%)
    pallas_call x1, Pallas kernels, body(): pl.pallas_call(functools.partial(kernel, rounds), in_specs=[pl.BlockSpec(...  51.9 us
    pallas_call x1, Pallas kernels, finished(): pl.pallas_call(finish, in_specs=[pl.BlockSpec(memory_space=pltpu.VMEM)] *...  1.16 us

profile of v7, /device:TPU:0, one launch (start us, length us, event | category | flops | bytes accessed | tf_op | source)
XLA Modules:
  0.0 53.9 jit_solution(6174421680602158723)
XLA Ops:
  0.6 51.9 %stratified_sgd.1 = (f32[512,256]{1,0:T(8,128)S(1)}, f32[1024,256]{1,0:T(8,128)S(1)}) custom-call(bf16[2,1024,256]{2,1,0:T(8,128)(2,1)} %bitcast.8, bf16[2,256,256]{2,1,0:T(8,128)(2,1)} %bitcast.9, s32[1,1024]{1,0:T(1,128)} %order_in.1, f32[512,256]{1,0:T(8,128)} %users_in.1, s32[16384,128]{1,0:T(8,128)} %bitcast.7), custom_call_target="tpu_custom_call" | custom-call | flops 9663676416 | bytes 12582912 | tf_op jit(solution)/shard_map/stratified_sgd/pallas_call | solution.py:368
  52.6 1.2 %finish.1 = (f32[512,256]{1,0:T(8,128)}, f32[1024,256]{1,0:T(8,128)}) custom-call(f32[512,256]{1,0:T(8,128)S(1)} %get-tuple-element.4.users_in, f32[1024,256]{1,0:T(8,128)S(1)} %get-tuple-element.5.items_in), custom_call_target="tpu_custom_call" | custom-call | tf_op jit(solution)/shard_map/finish/pallas_call | solution.py:346
